TPU v7x, 32 devices: a whole 2x2x4 slice. The times are simulated.
32 devices in a mesh: row: 8 (over z, x), col: 4 (over y, core).
Axes of the slice: x: 2, y: 2, z: 4, core: 2. Of those that a mesh axis runs over, the one named last changes fastest.
Arguments:
- panel_block: float32 [20480, 512], P('row', 'col'), may hold values from -12 to 12
- trailing: float32 [20480, 20480], P('row', 'col'), may hold values from -6 to 6
Outputs:
- updated: float32 [20480, 20480], P('row', 'col')
All inputs are finite; a program needn't handle non-finite values.
Results may differ from a plain program's by a relative error of at most 0.0003.
Values sent between devices are 32-bit elements; how exact they have to be, the bound alone decides.
No kernel may reach another device: no remote copies, remote signals or barrier semaphores. Data moves between devices by JAX's collectives and lax.ppermute only.
A program may use at most 192 MiB of HBM per device.

v0:
```python
import jax
import jax.numpy as jnp
from jax import lax
from jax.sharding import PartitionSpec as P

N = 20480


def on_device(panel_block, trailing):
    local_rows = panel_block.shape[0]
    local_width = panel_block.shape[1]
    rows_count = lax.axis_size("row")
    cols_count = lax.axis_size("col")
    copies = rows_count // cols_count
    row_owner = lax.axis_index("row")
    col_owner = lax.axis_index("col")
    mc_rows = lax.all_gather(panel_block, "col", axis=1, tiled=True)
    squares = lax.psum(jnp.sum(mc_rows * mc_rows), "row")
    column_block = lax.all_gather(panel_block, "row", axis=0, tiled=True)
    shaped = column_block.reshape(copies, cols_count, local_rows, local_width)
    moved = lax.all_to_all(shaped, "col", split_axis=1, concat_axis=3, tiled=True)
    stacked = moved.reshape(copies, local_rows, mc_rows.shape[1])
    mr_rows = jnp.transpose(stacked, (1, 0, 2)).reshape(copies * local_rows, stacked.shape[2])
    update = lax.dot_general(
        mc_rows,
        mr_rows,
        (((1,), (1,)), ((), ())),
        precision=lax.Precision.HIGHEST,
        preferred_element_type=jnp.float32,
    )
    row_index = jnp.arange(local_rows, dtype=jnp.int32) * rows_count + row_owner
    col_index = jnp.arange(mr_rows.shape[0], dtype=jnp.int32) * cols_count + col_owner
    lower_part = row_index[:, None] >= col_index[None, :]
    factor = 0.8 * jnp.sqrt(jnp.float32(N)) / jnp.sqrt(squares + 1e-06)
    return trailing - factor * jnp.where(lower_part, update, jnp.zeros_like(update))


def solution(mesh):
    in_specs = (P("row", "col"), P("row", "col"))
    out_specs = P("row", "col")
    return jax.shard_map(
        on_device, mesh=mesh, in_specs=in_specs, out_specs=out_specs, check_vma=False
    )
```

profile of v0, /device:TPU:0, one launch (start us, length us, event | category | flops | bytes accessed | tf_op | source)
XLA Modules:
  0.0 456.7 jit_solution(3020572873124051038)
XLA Ops:
  6.5 0.0 all-gather.5.cloned.1.call-start
  6.5 0.7 all-gather.5.cloned.1.call-update
  7.3 0.0 all-gather.3.cloned.1.call-start
  7.3 0.7 all-gather.3.cloned.1.call-update
  8.0 154.8 %all-gather.5.cloned.1.call-done = f32[20480,128]{1,0:T(8,128)} async-done(((f32[2560,128]{1,0:T(8,128)}), f32[20480,128]{1,0:T(8,128)}) %all-gather.5.cloned.1.call-update) | async-done | bytes 10485776 | tf_op jit(solution)/shard_map/all_gather | solution.py:19
  162.8 9.6 %copy.6 = f32[2,4,2560,128]{3,2,0,1:T(8,128)} copy(f32[2,4,2560,128]{3,2,1,0:T(8,128)} %bitcast.11) | data formatting | bytes 20971520 | tf_op jit(solution)/shard_map/reshape | solution.py:20
  172.4 6.0 %all-to-all-start = ((f32[2,4,2560,128]{3,2,0,1:T(8,128)}), f32[2,4,2560,128]{3,2,0,1:T(8,128)}, u32[]{:S(2)}, u32[]{:S(2)}) async-start(f32[2,4,2560,128]{3,2,0,1:T(8,128)} %copy.6), calls=%async_computation | async-start | bytes 20971520 | tf_op jit(solution)/shard_map/all_to_all | solution.py:21
  178.5 45.0 %all-gather.3.cloned.1.call-done = f32[2560,512]{1,0:T(8,128)} async-done(((f32[2560,128]{1,0:T(8,128)}), f32[2560,512]{1,0:T(8,128)}) %all-gather.3.cloned.1.call-update) | async-done | bytes 5242896 | tf_op jit(solution)/shard_map/all_gather | solution.py:17
  223.4 4.5 multiply_reduce_fusion
  227.9 25.2 %psum.7 = f32[]{:T(128)} all-reduce(f32[]{:T(128)} %multiply_reduce_fusion), channel_id=1, replica_groups=mesh['row'=8,'col'=4] {'row'}, use_global_device_ids=true, to_apply=%region_1.0 | all-reduce | flops 1 | bytes 8 | tf_op jit(solution)/shard_map/psum | solution.py:18
  253.8 60.0 %all-to-all-done = f32[2,4,2560,128]{3,2,0,1:T(8,128)} async-done(((f32[2,4,2560,128]{3,2,0,1:T(8,128)}), f32[2,4,2560,128]{3,2,0,1:T(8,128)}, u32[]{:S(2)}, u32[]{:S(2)}) %all-to-all-start) | async-done | bytes 10485792 | tf_op jit(solution)/shard_map/all_to_all | solution.py:21
  313.8 11.4 %copy.7 = f32[2,4,2560,128]{2,3,1,0:T(8,128)} copy(f32[2,4,2560,128]{3,2,0,1:T(8,128)} %all-to-all-done) | data formatting | bytes 20971520 | tf_op jit(solution)/shard_map/all_to_all | solution.py:21
  325.2 16.1 %copy.8 = f32[2560,2,512]{2,1,0:T(2,128)} copy(f32[2560,2,512]{0,2,1:T(8,128)} %bitcast.10) | data formatting | bytes 20971520 | tf_op jit(solution)/shard_map/transpose | solution.py:23
  341.3 13.3 %reshape.22 = f32[5120,512]{1,0:T(8,128)} reshape(f32[2560,2,512]{2,1,0:T(2,128)} %copy.8) | data formatting | bytes 20971520 | tf_op jit(solution)/shard_map/reshape | solution.py:23
  354.5 95.4 %multiply_subtract_fusion = f32[2560,5120]{1,0:T(8,128)} fusion(f32[2560,5120]{1,0:T(8,128)} %param.3, f32[2560,512]{1,0:T(8,128)} %all-gather.3.cloned.1.call-done, f32[5120,512]{1,0:T(8,128)} %reshape.22, s32[5120]{0:T(1024)S(1)} %multiply_add_fusion, f32[]{:T(128)S(6)} %div.3, s32[2560]{0:T(1024)S(1)} %multiply_add_fusion.1), kind=kOutput, calls=%fused_computation | convolution fusion | flops 80583065600 | bytes 120616960 | tf_op jit(solution)/shard_map/dot_general | solution.py:24
  (2 shorter events, 0.0 us)
Async XLA Ops:
  6.5 156.2 %all-gather.5.cloned.1.call-start = ((), (), s32[]{:S(2)}) async-start(), calls=%async_computation.2 | async-start | bytes 11796480 | tf_op jit(solution)/shard_map/all_gather | solution.py:19
  7.3 216.2 %all-gather.3.cloned.1.call-start = ((), (), s32[]{:S(2)}) async-start(), calls=%async_computation.1 | async-start | bytes 6553600 | tf_op jit(solution)/shard_map/all_gather | solution.py:17
  172.4 141.4 %all-to-all-start = ((f32[2,4,2560,128]{3,2,0,1:T(8,128)}), f32[2,4,2560,128]{3,2,0,1:T(8,128)}, u32[]{:S(2)}, u32[]{:S(2)}) async-start(f32[2,4,2560,128]{3,2,0,1:T(8,128)} %copy.6), calls=%async_computation | async-start | bytes 20971520 | tf_op jit(solution)/shard_map/all_to_all | solution.py:21
Sparse Core Ops, SparseCore 0:
  9.5 153.2 all-gather.4
  164.3 59.0 all-gather.2
where the time goes:
time: 458 us; the launch traced here: 457 us
  waiting for transfers between devices  261 us (57%)
  matrix products  95.4 us (21%)
  local copies, waits for them, and re-layouts  50.4 us (11%)
  blocking collectives  25.2 us (6%)
  between operations  14.1 us (3%)
  starting transfers between devices  6.08 us (1%)
    all_gather x1, waiting for transfers between devices, on_device(): column_block = lax.all_gather(panel_block, 'row', axis=0, tiled=True)  155 us
    dot_general x1, matrix products, on_device(): lax.dot_general(mc_rows, mr_rows, (((1,), (1,)), ((), ())), precision=lax...  95.4 us
    all_to_all x1, waiting for transfers between devices, on_device(): lax.all_to_all(shaped, 'col', split_axis=1, concat_axis=3, tiled=True)  60 us
    all_gather x1, waiting for transfers between devices, on_device(): mc_rows = lax.all_gather(panel_block, 'col', axis=1, tiled=True)  45 us
    psum x1, blocking collectives, on_device(): squares = lax.psum(jnp.sum(mc_rows * mc_rows), 'row')  25.2 us
    transpose x1, local copies, waits for them, and re-layouts, on_device(): jnp.transpose(stacked, (1, 0, 2))  16.1 us
    reshape x1, local copies, waits for them, and re-layouts, on_device(): jnp.transpose(stacked, (1, 0, 2))  13.3 us
    all_to_all x1, local copies, waits for them, and re-layouts, on_device(): lax.all_to_all(shaped, 'col', split_axis=1, concat_axis=3, tiled=True)  11.4 us
  transfers between devices with their start and end apart: 3, of which 3 were waited for; matrix products, arithmetic and copies ran while one was open for 3% of the time, Pallas kernels for 0%

commit v1 on v0

--- a/solution.py
+++ b/solution.py
@@ -4,6 +4,17 @@
 from jax.sharding import PartitionSpec as P
 
 N = 20480
+
+
+def turned_line(block, axis, d):
+    size = lax.axis_size(axis)
+    right = [(i, (i + 1) % size) for i in range(size)]
+    parts = [block]
+    for far in range(1, size):
+        parts = [lax.ppermute(parts[0], axis, right), *parts]
+    out = jnp.concatenate(parts, axis=d)
+    shift = (lax.axis_index(axis) + 1) * parts[-1].shape[d]
+    return jnp.roll(out, shift, axis=d)
 
 
 def on_device(panel_block, trailing):
@@ -16,7 +27,7 @@
     col_owner = lax.axis_index("col")
     mc_rows = lax.all_gather(panel_block, "col", axis=1, tiled=True)
     squares = lax.psum(jnp.sum(mc_rows * mc_rows), "row")
-    column_block = lax.all_gather(panel_block, "row", axis=0, tiled=True)
+    column_block = turned_line(panel_block, "row", 0)
     shaped = column_block.reshape(copies, cols_count, local_rows, local_width)
     moved = lax.all_to_all(shaped, "col", split_axis=1, concat_axis=3, tiled=True)
     stacked = moved.reshape(copies, local_rows, mc_rows.shape[1])

time: 458 us -> 568 us (1.24)
  local copies, waits for them, and re-layouts: 50.4 us -> 168 us
  blocking collectives: 25.2 us -> 17.8 us
    ppermute x0 -> x7, waiting for transfers between devices: none -> 215 us  [turned_line(): parts = [lax.ppermute(parts[0], axis, right), *parts]]
    all_gather x1 -> x0, waiting for transfers between devices: 155 us -> none  [on_device(): column_block = lax.all_gather(panel_block, 'row', axis=0, tiled=True)]
    unnamed x0 -> x34, local copies, waits for them, and re-layouts: none -> 69.5 us
    sub x0 -> x1, local copies, waits for them, and re-layouts: none -> 52 us  [on_device(): trailing - factor * jnp.where(lower_part, update, jnp.zeros_like(update))]
    all_gather x1, waiting for transfers between devices: 45 us -> 0.02 us  [on_device(): mc_rows = lax.all_gather(panel_block, 'col', axis=1, tiled=True)]
    all_to_all x1, waiting for transfers between devices: 60 us -> 40.5 us  [on_device(): lax.all_to_all(shaped, 'col', split_axis=1, concat_axis=3, tiled=True)]
    psum x1, blocking collectives: 25.2 us -> 17.8 us  [on_device(): squares = lax.psum(jnp.sum(mc_rows * mc_rows), 'row')]
  transfers between devices with their start and end apart: 3 -> 9, of which waited for: 3 -> 8; matrix products, arithmetic and copies ran while one was open for 3% -> 13% of each run, Pallas kernels for 0% -> 0%
where the time goes in v1:
time: 568 us; the launch traced here: 565 us
  waiting for transfers between devices  256 us (45%)
  local copies, waits for them, and re-layouts  168 us (30%)
  matrix products  95.4 us (17%)
  blocking collectives  17.8 us (3%)
  between operations  14.4 us (3%)
  starting transfers between devices  8.97 us (2%)
    ppermute x7, waiting for transfers between devices, turned_line(): parts = [lax.ppermute(parts[0], axis, right), *parts]  215 us
    dot_general x1, matrix products, on_device(): lax.dot_general(mc_rows, mr_rows, (((1,), (1,)), ((), ())), precision=lax...  95.4 us
    unnamed x34, local copies, waits for them, and re-layouts  69.5 us
    sub x1, local copies, waits for them, and re-layouts, on_device(): trailing - factor * jnp.where(lower_part, update, jnp.zeros_like(update))  52 us
    all_to_all x1, waiting for transfers between devices, on_device(): lax.all_to_all(shaped, 'col', split_axis=1, concat_axis=3, tiled=True)  40.5 us
    psum x1, blocking collectives, on_device(): squares = lax.psum(jnp.sum(mc_rows * mc_rows), 'row')  17.8 us
    transpose x1, local copies, waits for them, and re-layouts, on_device(): jnp.transpose(stacked, (1, 0, 2))  16.1 us
    reshape x1, local copies, waits for them, and re-layouts, on_device(): jnp.transpose(stacked, (1, 0, 2))  13.2 us
  transfers between devices with their start and end apart: 9, of which 8 were waited for; matrix products, arithmetic and copies ran while one was open for 13% of the time, Pallas kernels for 0%

profile of v1, /device:TPU:0, one launch (start us, length us, event | category | flops | bytes accessed | tf_op | source)
XLA Modules:
  0.0 564.9 jit_solution(18077770429059884299)
XLA Ops:
  6.5 0.0 copy-start
  6.5 0.0 all-gather.2.cloned.1.call-start
  6.5 3.0 collective-permute-start
  9.5 32.1 %collective-permute-done = f32[2560,128]{1,0:T(8,128)S(1)} collective-permute-done((f32[2560,128]{1,0:T(8,128)}, f32[2560,128]{1,0:T(8,128)S(1)}, u32[]{:S(2)}, u32[]{:S(2)}) %collective-permute-start) | collective-permute-done | bytes 1310752 | tf_op jit(solution)/shard_map/ppermute | solution.py:14
  41.6 0.0 collective-permute-start.1
  41.6 32.6 %collective-permute-done.1 = f32[2560,128]{1,0:T(8,128)S(1)} collective-permute-done((f32[2560,128]{1,0:T(8,128)S(1)}, f32[2560,128]{1,0:T(8,128)S(1)}, u32[]{:S(2)}, u32[]{:S(2)}) %collective-permute-start.1) | collective-permute-done | bytes 1310752 | tf_op jit(solution)/shard_map/ppermute | solution.py:14
  74.2 0.0 copy-start.1
  74.2 1.1 copy-done.1
  75.3 0.0 collective-permute-start.2
  75.3 31.8 %collective-permute-done.2 = f32[2560,128]{1,0:T(8,128)S(1)} collective-permute-done((f32[2560,128]{1,0:T(8,128)S(1)}, f32[2560,128]{1,0:T(8,128)S(1)}, u32[]{:S(2)}, u32[]{:S(2)}) %collective-permute-start.2) | collective-permute-done | bytes 1310752 | tf_op jit(solution)/shard_map/ppermute | solution.py:14
  107.1 0.0 copy-start.3
  107.1 1.1 copy-done.3
  108.2 0.0 collective-permute-start.3
  108.2 30.9 %collective-permute-done.3 = f32[2560,128]{1,0:T(8,128)S(1)} collective-permute-done((f32[2560,128]{1,0:T(8,128)S(1)}, f32[2560,128]{1,0:T(8,128)S(1)}, u32[]{:S(2)}, u32[]{:S(2)}) %collective-permute-start.3) | collective-permute-done | bytes 1310752 | tf_op jit(solution)/shard_map/ppermute | solution.py:14
  139.1 0.0 copy-start.5
  139.1 1.1 copy-done.5
  140.1 0.0 collective-permute-start.4
  140.1 30.1 %collective-permute-done.4 = f32[2560,128]{1,0:T(8,128)S(1)} collective-permute-done((f32[2560,128]{1,0:T(8,128)S(1)}, f32[2560,128]{1,0:T(8,128)S(1)}, u32[]{:S(2)}, u32[]{:S(2)}) %collective-permute-start.4) | collective-permute-done | bytes 1310752 | tf_op jit(solution)/shard_map/ppermute | solution.py:14
  170.2 0.0 copy-start.7
  170.2 1.1 copy-done.7
  171.3 0.0 collective-permute-start.5
  171.3 29.3 %collective-permute-done.5 = f32[2560,128]{1,0:T(8,128)} collective-permute-done((f32[2560,128]{1,0:T(8,128)S(1)}, f32[2560,128]{1,0:T(8,128)}, u32[]{:S(2)}, u32[]{:S(2)}) %collective-permute-start.5) | collective-permute-done | bytes 1310752 | tf_op jit(solution)/shard_map/ppermute | solution.py:14
  200.6 0.0 collective-permute-start.6
  200.6 0.0 all-gather.2.cloned.1.call-update
  200.7 0.0 copy-start.8
  200.7 0.0 copy-start.6
  200.7 0.0 copy-start.4
  200.7 0.0 copy-start.2
  200.7 28.6 %collective-permute-done.6 = f32[2560,128]{1,0:T(8,128)} collective-permute-done((f32[2560,128]{1,0:T(8,128)}, f32[2560,128]{1,0:T(8,128)}, u32[]{:S(2)}, u32[]{:S(2)}) %collective-permute-start.6) | collective-permute-done | bytes 1310752 | tf_op jit(solution)/shard_map/ppermute | solution.py:14
  229.3 1.4 constant_dynamic-update-slice_fusion.15
  230.7 1.4 constant_dynamic-update-slice_fusion.14
  232.1 1.4 constant_dynamic-update-slice_fusion.13
  233.5 1.4 constant_dynamic-update-slice_fusion.12
  234.9 1.4 constant_dynamic-update-slice_fusion.11
  236.3 1.4 constant_dynamic-update-slice_fusion.10
  237.7 0.1 constant_dynamic-update-slice_fusion.9
  237.8 1.4 constant_dynamic-update-slice_fusion.8
  239.2 1.4 constant_dynamic-update-slice_fusion.7
  240.6 1.5 constant_dynamic-update-slice_fusion.6
  242.1 0.0 copy-done.8
  242.1 0.1 constant_dynamic-update-slice_fusion.5
  242.2 0.0 copy-done.6
  242.2 0.1 constant_dynamic-update-slice_fusion.4
  242.3 0.0 copy-done.4
  242.3 0.1 constant_dynamic-update-slice_fusion.3
  242.4 0.0 copy-done.2
  242.4 0.1 constant_dynamic-update-slice_fusion.2
  242.5 0.1 constant_dynamic-update-slice_fusion.1
  242.6 0.0 copy-done
  242.6 0.1 constant_dynamic-update-slice_fusion
  242.7 0.9 constant_dynamic-slice_fusion
  243.6 4.5 copy.12
  248.2 6.0 %all-to-all-start = ((f32[2,4,2560,128]{3,2,0,1:T(8,128)}), f32[2,4,2560,128]{3,2,0,1:T(8,128)}, u32[]{:S(2)}, u32[]{:S(2)}) async-start(f32[2,4,2560,128]{3,2,0,1:T(8,128)} %copy.12), calls=%async_computation | async-start | bytes 20971520 | tf_op jit(solution)/shard_map/all_to_all | solution.py:32
  254.2 0.0 all-gather.2.cloned.1.call-done
  254.2 4.5 multiply_reduce_fusion
  258.7 52.0 %copy.15 = f32[2560,5120]{0,1:T(8,128)} copy(f32[2560,5120]{1,0:T(8,128)} %param.3) | data formatting | bytes 104857600 | tf_op args[1]
  310.8 17.8 %psum.7 = f32[]{:T(128)} all-reduce(f32[]{:T(128)} %multiply_reduce_fusion), channel_id=1, replica_groups=mesh['row'=8,'col'=4] {'row'}, use_global_device_ids=true, to_apply=%region_1.0 | all-reduce | flops 1 | bytes 8 | tf_op jit(solution)/shard_map/psum | solution.py:29
  329.3 40.5 %all-to-all-done = f32[2,4,2560,128]{3,2,0,1:T(8,128)} async-done(((f32[2,4,2560,128]{3,2,0,1:T(8,128)}), f32[2,4,2560,128]{3,2,0,1:T(8,128)}, u32[]{:S(2)}, u32[]{:S(2)}) %all-to-all-start) | async-done | bytes 10485792 | tf_op jit(solution)/shard_map/all_to_all | solution.py:32
  369.8 11.5 %copy.13 = f32[2,4,2560,128]{2,3,1,0:T(8,128)} copy(f32[2,4,2560,128]{3,2,0,1:T(8,128)} %all-to-all-done) | data formatting | bytes 20971520 | tf_op jit(solution)/shard_map/all_to_all | solution.py:32
  381.2 16.1 %copy.14 = f32[2560,2,512]{2,1,0:T(2,128)} copy(f32[2560,2,512]{0,2,1:T(8,128)} %bitcast.17) | data formatting | bytes 20971520 | tf_op jit(solution)/shard_map/transpose | solution.py:34
  397.4 13.2 %reshape.22 = f32[5120,512]{1,0:T(8,128)} reshape(f32[2560,2,512]{2,1,0:T(2,128)} %copy.14) | data formatting | bytes 20971520 | tf_op jit(solution)/shard_map/reshape | solution.py:34
  410.6 95.4 %fusion.1 = f32[2560,5120]{0,1:T(8,128)} fusion(f32[2560,5120]{0,1:T(8,128)} %copy.15, f32[5120,512]{1,0:T(8,128)} %reshape.22, f32[2560,512]{1,0:T(8,128)} %all-gather.2.cloned.1.call-done, s32[2560]{0:T(1024)S(1)} %multiply_add_fusion.1, f32[]{:T(128)S(6)} %div.3, s32[5120]{0:T(1024)S(1)} %multiply_add_fusion), kind=kOutput, calls=%fused_computation.2 | convolution fusion | flops 80583065600 | bytes 120616960 | tf_op jit(solution)/shard_map/dot_general | solution.py:35
  506.0 52.0 %copy.16 = f32[2560,5120]{1,0:T(8,128)} copy(f32[2560,5120]{0,1:T(8,128)} %fusion.1) | data formatting | bytes 104857600 | tf_op jit(solution)/shard_map/sub | solution.py:46
  (2 shorter events, 0.0 us)
Async XLA Ops:
  6.5 236.1 %copy-start = (f32[2560,128]{1,0:T(8,128)S(1)}, f32[2560,128]{1,0:T(8,128)}, u32[]{:S(2)}) copy-start(f32[2560,128]{1,0:T(8,128)} %param.2) | copy-start | bytes 3932164
  6.5 247.7 %all-gather.2.cloned.1.call-start = ((), (), s32[]{:S(2)}) async-start(), calls=%async_computation.1 | async-start | bytes 6553600 | tf_op jit(solution)/shard_map/all_gather | solution.py:28
  6.5 35.1 %collective-permute-start = (f32[2560,128]{1,0:T(8,128)}, f32[2560,128]{1,0:T(8,128)S(1)}, u32[]{:S(2)}, u32[]{:S(2)}) collective-permute-start(f32[2560,128]{1,0:T(8,128)} %param.2), channel_id=1, source_target_pairs={{0,4},{4,8},{8,12},{12,16},{16,20},{20,24},{24,28},{28,0},{1,5},{5... | collective-permute-start | bytes 3932168 | tf_op jit(solution)/shard_map/ppermute | solution.py:14
  41.6 32.6 %collective-permute-start.1 = (f32[2560,128]{1,0:T(8,128)S(1)}, f32[2560,128]{1,0:T(8,128)S(1)}, u32[]{:S(2)}, u32[]{:S(2)}) collective-permute-start(f32[2560,128]{1,0:T(8,128)S(1)} %collective-permute-done), channel_id=1, source_target_pairs={{0,4},{4,8},{8,12},{12,16},{16,20},{20,24},{24,28},{28,0},{1,5},{5... | collective-permute-start | bytes 3932168 | tf_op jit(solution)/shard_map/ppermute | solution.py:14
  74.2 1.1 copy-start.1
  75.3 31.8 %collective-permute-start.2 = (f32[2560,128]{1,0:T(8,128)S(1)}, f32[2560,128]{1,0:T(8,128)S(1)}, u32[]{:S(2)}, u32[]{:S(2)}) collective-permute-start(f32[2560,128]{1,0:T(8,128)S(1)} %collective-permute-done.1), channel_id=1, source_target_pairs={{0,4},{4,8},{8,12},{12,16},{16,20},{20,24},{24,28},{28,0},{1,5},{5... | collective-permute-start | bytes 3932168 | tf_op jit(solution)/shard_map/ppermute | solution.py:14
  107.1 1.1 copy-start.3
  108.2 30.9 %collective-permute-start.3 = (f32[2560,128]{1,0:T(8,128)S(1)}, f32[2560,128]{1,0:T(8,128)S(1)}, u32[]{:S(2)}, u32[]{:S(2)}) collective-permute-start(f32[2560,128]{1,0:T(8,128)S(1)} %collective-permute-done.2), channel_id=1, source_target_pairs={{0,4},{4,8},{8,12},{12,16},{16,20},{20,24},{24,28},{28,0},{1,5},{5... | collective-permute-start | bytes 3932168 | tf_op jit(solution)/shard_map/ppermute | solution.py:14
  139.1 1.1 copy-start.5
  140.1 30.1 %collective-permute-start.4 = (f32[2560,128]{1,0:T(8,128)S(1)}, f32[2560,128]{1,0:T(8,128)S(1)}, u32[]{:S(2)}, u32[]{:S(2)}) collective-permute-start(f32[2560,128]{1,0:T(8,128)S(1)} %collective-permute-done.3), channel_id=1, source_target_pairs={{0,4},{4,8},{8,12},{12,16},{16,20},{20,24},{24,28},{28,0},{1,5},{5... | collective-permute-start | bytes 3932168 | tf_op jit(solution)/shard_map/ppermute | solution.py:14
  170.2 1.1 copy-start.7
  171.3 29.3 %collective-permute-start.5 = (f32[2560,128]{1,0:T(8,128)S(1)}, f32[2560,128]{1,0:T(8,128)}, u32[]{:S(2)}, u32[]{:S(2)}) collective-permute-start(f32[2560,128]{1,0:T(8,128)S(1)} %collective-permute-done.4), channel_id=1, source_target_pairs={{0,4},{4,8},{8,12},{12,16},{16,20},{20,24},{24,28},{28,0},{1,5},{5... | collective-permute-start | bytes 3932168 | tf_op jit(solution)/shard_map/ppermute | solution.py:14
  200.6 28.7 %collective-permute-start.6 = (f32[2560,128]{1,0:T(8,128)}, f32[2560,128]{1,0:T(8,128)}, u32[]{:S(2)}, u32[]{:S(2)}) collective-permute-start(f32[2560,128]{1,0:T(8,128)} %collective-permute-done.5), channel_id=1, source_target_pairs={{0,4},{4,8},{8,12},{12,16},{16,20},{20,24},{24,28},{28,0},{1,5},{5... | collective-permute-start | bytes 3932168 | tf_op jit(solution)/shard_map/ppermute | solution.py:14
  200.7 41.5 %copy-start.8 = (f32[2560,128]{1,0:T(8,128)S(1)}, f32[2560,128]{1,0:T(8,128)}, u32[]{:S(2)}) copy-start(f32[2560,128]{1,0:T(8,128)} %copy-done.7) | copy-start | bytes 3932164
  200.7 41.6 %copy-start.6 = (f32[2560,128]{1,0:T(8,128)S(1)}, f32[2560,128]{1,0:T(8,128)}, u32[]{:S(2)}) copy-start(f32[2560,128]{1,0:T(8,128)} %copy-done.5) | copy-start | bytes 3932164
  200.7 41.7 %copy-start.4 = (f32[2560,128]{1,0:T(8,128)S(1)}, f32[2560,128]{1,0:T(8,128)}, u32[]{:S(2)}) copy-start(f32[2560,128]{1,0:T(8,128)} %copy-done.3) | copy-start | bytes 3932164
  200.7 41.7 %copy-start.2 = (f32[2560,128]{1,0:T(8,128)S(1)}, f32[2560,128]{1,0:T(8,128)}, u32[]{:S(2)}) copy-start(f32[2560,128]{1,0:T(8,128)} %copy-done.1) | copy-start | bytes 3932164
  248.2 121.6 %all-to-all-start = ((f32[2,4,2560,128]{3,2,0,1:T(8,128)}), f32[2,4,2560,128]{3,2,0,1:T(8,128)}, u32[]{:S(2)}, u32[]{:S(2)}) async-start(f32[2,4,2560,128]{3,2,0,1:T(8,128)} %copy.12), calls=%async_computation | async-start | bytes 20971520 | tf_op jit(solution)/shard_map/all_to_all | solution.py:32
Sparse Core Ops, SparseCore 0:
  200.7 41.8 all-gather.1
